TPU v7x, 128 devices: a whole 4x4x4 slice. The times are simulated.
128 devices in a mesh: gx: 16 (over y, x), gy: 8 (over z, core).
Axes of the slice: x: 4, y: 4, z: 4, core: 2. Of those that a mesh axis runs over, the one named last changes fastest.
Arguments:
- source_field: bfloat16 [16384, 128, 128], P(('gx', 'gy')), may hold values from -6 to 6
- weight_blocks: bfloat16 [65536, 128, 128], P(('gx', 'gy')), may hold values from -0.1875 to 0.1875
- source_ids: int32 [65536], replicated, may hold values from 0 to 16383, as said below
- target_ids: int32 [65536], replicated, may hold values from 0 to 8191, as said below
Outputs:
- remapped: bfloat16 [8192, 128, 128], P(('gx', 'gy'))
Inputs may be any that keep to these rules, and one draw needn't show every extreme that they name: `source_ids`: source block b lies on device b // 128 of gx+gy, and weight block k lies on device k // 512. The weight blocks of device d name only source blocks of devices d - 2 to d + 2. Among the weight blocks of one device, at most 64 distinct source blocks of any one other device are named, and exactly 64 for some other device. `target_ids`: target block t lies on device t // 64 of gx+gy. The weight blocks of device d name only target blocks of devices d - 2 to d + 2. Among the weight blocks of one device, at most 16 distinct target blocks of any one device are named, and exactly 16 for some other device.
All inputs are finite; a program needn't handle non-finite values.
Results may differ from a plain program's by a relative error of at most 0.001.
Values may be sent and summed in bfloat16 or wider, within the bound.
A program may use at most 192 MiB of HBM per device.

v0:
```python
import functools

import jax
import jax.numpy as jnp
from jax import lax
from jax.experimental import pallas as pl
from jax.experimental.pallas import tpu as pltpu
from jax.sharding import PartitionSpec as P


BLK = 128
SB = 128
TB = 64
WB = 512
CS = 64
CT = 16
AXES = ("gx", "gy")
TRASH = 80
SLOTS = 84
GROUP = 16
PART = 54
PART_B = 52
UNION = PART + PART_B
TAIL = SB - UNION
FAR = 44
REST = CS - FAR
HEADS = 6
VLIM = 9
CHUNKS = 8
HALF_ROWS = CT // 2 * BLK + 16


f32 = jnp.float32
i32 = jnp.int32
bf16 = jnp.bfloat16


def iota(dim):
    return lax.broadcasted_iota(i32, (BLK, BLK), dim)


def presence(rows, base, limit):
    sub = iota(0)
    hits = jnp.zeros((BLK, BLK), f32)
    for q in range(4):
        hits = hits + (jnp.broadcast_to(rows[q : q + 1, :] - base, (BLK, BLK)) == sub).astype(f32)
    count = jnp.dot(hits.astype(bf16), jnp.ones((BLK, BLK), bf16), preferred_element_type=f32)
    return ((count > 0.5) & (sub < limit)).astype(f32)


def ranks(present):
    lower = (iota(1) < iota(0)).astype(bf16)
    return jnp.dot(lower, present.astype(bf16), preferred_element_type=f32)


def listed(present, rank, fill):
    sel = (present > 0.5) & (rank == iota(1).astype(f32))
    found = jnp.sum(sel.astype(f32), axis=0, keepdims=True)
    index = jnp.sum(jnp.where(sel, iota(0).astype(f32), 0.0), axis=0, keepdims=True)
    return jnp.where(found > 0.5, index, fill).astype(i32)


def ranked(rows, base, rank):
    out = []
    for q in range(4):
        sel = jnp.broadcast_to(rows[q : q + 1, :] - base, (BLK, BLK)) == iota(0)
        out.append(jnp.sum(jnp.where(sel, rank, 0.0), axis=0, keepdims=True))
    return jnp.concatenate(out, axis=0).astype(i32)


def gather_ids(n, me, refs, sems):
    loads = []
    for i, (ids, ids_v) in enumerate(refs):
        for r in range(5):
            e = jnp.clip(me + (r - 2), 0, n - 1)
            loads.append(pltpu.make_async_copy(ids.at[e], ids_v.at[r], sems.at[5 * i + r]))
    for c in loads:
        c.start()
    for c in loads:
        c.wait()


def pack(src_v, list_s, row, first, out, count):
    def move(r, carry):
        for u in range(2):
            out[r * 2 + u] = src_v[list_s[row, first + r * 2 + u]]
        return carry

    lax.fori_loop(0, count // 2, move, 0)


def either(one, other, base):
    return jnp.maximum(presence(one, base, SB), presence(other, base, SB))


def union_kernel(n, sids, src, pn, sid_v, src_v, list_v, list_s, sems):
    me = lax.axis_index(AXES)
    side = 1 - 2 * (me % 2)
    loads = []
    for r in (2 - side, 2 - 2 * side):
        e = jnp.clip(me + (r - 2), 0, n - 1)
        loads.append(pltpu.make_async_copy(sids.at[e], sid_v.at[r], sems.at[len(loads)]))
        loads[-1].start()
    fetch = pltpu.make_async_copy(src, src_v, sems.at[10])
    fetch.start()
    for x in loads:
        x.wait()
    base = me * SB
    present = either(sid_v[2 - side], sid_v[2 - 2 * side], base)
    list_v[...] = listed(present, ranks(present), 0.0)
    move = pltpu.make_async_copy(list_v, list_s, sems.at[11])
    move.start()
    move.wait()
    fetch.wait()

    def send(r, carry):
        for u in range(6):
            b = list_s[0, r * 6 + u]
            pltpu.make_async_copy(src_v.at[b], pn.at[r * 6 + u], sems.at[2]).start()
        return carry

    lax.fori_loop(0, PART // 6, send, 0)
    pltpu.make_async_copy(src_v.at[pl.ds(0, PART)], pn, sems.at[2]).wait()


def plan_kernel(n, sids, tids, src_v, py, px, pz, pd, pt, plan, recv, sid_v, tid_v, list_v, list_s, sems):
    me = lax.axis_index(AXES)
    side = 1 - 2 * (me % 2)
    gather_ids(n, me, ((sids, sid_v), (tids, tid_v)), sems)
    base = me * SB
    for f, rel in enumerate((2 * side, side)):
        present = presence(sid_v[2 + rel], base, SB)
        list_v[f : f + 1, :] = listed(present, ranks(present), 0.0)
    present = either(sid_v[2 - side], sid_v[2 - 2 * side], base)
    list_v[2:3, :] = listed(present, ranks(present), 0.0)
    move = pltpu.make_async_copy(list_v, list_s, sems.at[11])
    move.start()

    own = sid_v[2]
    rel_of = own // SB - me
    pos = own - me * SB
    group = jnp.zeros((4, BLK), i32)
    for c, rel in ((6, -2 * side), (3, side)):
        base = (me + rel) * SB
        rank = ranked(own, base, ranks(presence(own, base, SB)))
        here = rel_of == rel
        late = (rank >= FAR) & (c == 6)
        pos = jnp.where(here, jnp.where(late, rank - FAR, rank), pos)
        group = jnp.where(here, jnp.where(late, 9, c), group)
    for lo, hi, over, rel in ((1, 5, 7, -side), (2, 4, 8, 2 * side)):
        base = (me + rel) * SB
        rank = ranked(own, base, ranks(either(own, sid_v[2 + side], base)))
        here = rel_of == rel
        part = (rank >= PART).astype(i32) + (rank >= UNION).astype(i32)
        pos = jnp.where(here, rank - jnp.where(part == 0, 0, jnp.where(part == 1, PART, UNION)), pos)
        group = jnp.where(here, jnp.where(part == 0, lo, jnp.where(part == 1, hi, over)), group)
    town = tid_v[2]
    trel = town // TB - me
    slot = jnp.zeros((4, BLK), i32)
    for f, rel in enumerate((0, 2 * side, -2 * side, side, -side)):
        base = (me + rel) * TB
        rank = ranked(town, base, ranks(presence(town, base, TB)))
        slot = jnp.where(trel == rel, rank + f * CT, slot)
    k = lax.broadcasted_iota(i32, (4, BLK), 0) * BLK + lax.broadcasted_iota(i32, (4, BLK), 1)
    entry = k + pos * 512 + slot * (1 << 16)

    upper = (iota(0) <= iota(1)).astype(bf16)
    dest = jnp.zeros((4, BLK), f32)
    start = jnp.zeros((1, 1), f32)
    heads = jnp.zeros((1, BLK), f32)
    lane = lax.broadcasted_iota(i32, (1, BLK), 1)
    for c in range(10):
        here = (group == c).astype(f32)
        run = jnp.dot(here.astype(bf16), upper, preferred_element_type=f32)
        rows = []
        total = jnp.zeros((1, 1), f32)
        for q in range(4):
            rows.append(run[q : q + 1, :] + total)
            total = total + run[q : q + 1, BLK - 1 : BLK]
        dest = jnp.where(here > 0.5, start + jnp.concatenate(rows, axis=0) - 1.0, dest)
        groups = jnp.floor((total + (GROUP - 1)) * (1.0 / GROUP))
        heads = jnp.where(lane == c, start, heads)
        heads = jnp.where(lane == 16 + c, groups, heads)
        start = start + groups * GROUP
    cols_d = jnp.transpose(jnp.concatenate([dest, entry.astype(f32)], axis=0))
    for p in range(HEADS):
        at = (iota(1) + p * BLK).astype(f32)
        best = jnp.zeros((1, BLK), f32)
        seen = jnp.zeros((1, BLK), f32)
        for q in range(4):
            hit = jnp.broadcast_to(cols_d[:, q : q + 1], (BLK, BLK)) == at
            val = jnp.broadcast_to(cols_d[:, 4 + q : 5 + q], (BLK, BLK))
            best = best + jnp.sum(jnp.where(hit, val, 0.0), axis=0, keepdims=True)
            seen = seen + jnp.sum(hit.astype(f32), axis=0, keepdims=True)
        plan[p : p + 1, :] = jnp.where(seen > 0.5, best, float(TRASH << 16)).astype(i32)
    plan[HEADS : HEADS + 1, :] = heads.astype(i32)

    for f, rel in enumerate((0, -2 * side, 2 * side, side, -side)):
        present = presence(tid_v[2 + rel], me * TB, TB)
        e = me + rel
        present = jnp.where((e >= 0) & (e < n), present, 0.0)
        recv[f : f + 1, :] = listed(present, ranks(present), float(TB))

    move.wait()
    pack(src_v, list_s, 2, PART, py, PART_B)
    pack(src_v, list_s, 0, 0, px, FAR)
    pack(src_v, list_s, 0, FAR, pz, REST)
    pack(src_v, list_s, 1, 0, pd, CS)
    pack(src_v, list_s, 2, UNION, pt, TAIL)


def excess_kernel(ids, flag):
    sub = lax.broadcasted_iota(i32, (8, BLK), 0)
    lane = lax.broadcasted_iota(i32, (8, BLK), 1)
    even = lane % 2 == 0
    owners = [lane - lane % 2 - 1, lane - lane % 2 + 2]
    bits = [[jnp.zeros((8, BLK), i32) for _ in range(4)] for _ in range(2)]
    for q in range(4):
        turned = jnp.transpose(ids[:, q, :].astype(f32)).astype(i32)
        for r in range(BLK // 8):
            rows = turned[r * 8 : r * 8 + 8, :]
            for o in range(2):
                local = rows - owners[o] * SB
                word = local >> 5
                bit = jnp.left_shift(jnp.ones_like(local), local & 31)
                for v in range(4):
                    bits[o][v] = bits[o][v] | jnp.where(word == v, bit, 0)
    worst = sub * 0
    for o in range(2):
        total = sub * 0
        for v in range(4):
            x = bits[o][v]
            for step in (4, 2, 1):
                x = x | pltpu.roll(x, step, 0)
            x = x | jnp.where(even, pltpu.roll(x, BLK - 1, 1), pltpu.roll(x, 1, 1))
            total = total + lax.population_count(x)
        worst = jnp.maximum(worst, total)
    worst = jnp.max(worst.astype(f32), axis=1, keepdims=True)
    flag[...] = jnp.broadcast_to((worst > UNION).astype(i32), (8, BLK))


any_spec = pl.BlockSpec(memory_space=pltpu.HBM)
sm_spec = pl.BlockSpec(memory_space=pltpu.SMEM)
vm_spec = pl.BlockSpec(memory_space=pltpu.VMEM)


def blocks(count):
    return jax.ShapeDtypeStruct((count, BLK, BLK), bf16)


def cost(flops):
    return pl.CostEstimate(flops=flops, bytes_accessed=8_000_000, transcendentals=0)


def index_scratch(*more):
    return [
        *more,
        pltpu.VMEM((8, BLK), i32),
        pltpu.SMEM((8, BLK), i32),
        pltpu.SemaphoreType.DMA((12,)),
    ]


def limit(mib):
    return pltpu.CompilerParams(vmem_limit_bytes=mib * 1024 * 1024)


def call_union(n, sids, src):
    return pl.pallas_call(
        functools.partial(union_kernel, n),
        out_shape=blocks(PART),
        in_specs=[any_spec] * 2,
        out_specs=any_spec,
        scratch_shapes=[
            pltpu.VMEM((5, 4, BLK), i32),
            pltpu.VMEM((SB, BLK, BLK), bf16),
            pltpu.VMEM((1, BLK), i32),
            pltpu.SMEM((1, BLK), i32),
            pltpu.SemaphoreType.DMA((12,)),
        ],
        name="union",
        cost_estimate=cost(1_000_000),
    )(sids, src)


def call_plan(n, sids, tids, src):
    table = jax.ShapeDtypeStruct((8, BLK), i32)
    return pl.pallas_call(
        functools.partial(plan_kernel, n),
        out_shape=[blocks(c) for c in (PART_B, FAR, REST, CS, TAIL)] + [table] * 2,
        in_specs=[any_spec, any_spec, vm_spec],
        out_specs=[vm_spec] * 7,
        scratch_shapes=index_scratch(*[pltpu.VMEM((5, 4, BLK), i32)] * 2),
        name="plan",
        compiler_params=limit(16),
        cost_estimate=cost(500_000_000),
    )(sids, tids, src)


def call_excess(ids):
    return pl.pallas_call(
        excess_kernel,
        out_shape=jax.ShapeDtypeStruct((8, BLK), i32),
        in_specs=[vm_spec],
        out_specs=vm_spec,
        name="excess",
        compiler_params=limit(4),
        cost_estimate=cost(500_000_000),
    )(ids)


def products(plan, cls, w, tab, acc):
    first = plan[HEADS, cls]

    def step(g, carry):
        parts = []
        slots = []
        for u in range(GROUP):
            at = first + g * GROUP + u
            entry = plan[at >> 7, at & 127]
            slots.append(entry >> 16)
            parts.append(jnp.dot(w[entry & 511], tab[(entry >> 9) & 127], preferred_element_type=f32))
        for u in range(GROUP):
            acc[slots[u]] = acc[slots[u]] + parts[u]
        return carry

    lax.fori_loop(0, plan[HEADS, 16 + cls], step, 0)


def first_kernel(plan, w_hbm, src, acc, w, sems):
    step = WB // CHUNKS
    loads = []
    for i in range(CHUNKS):
        at = pl.ds(i * step, step)
        loads.append(pltpu.make_async_copy(w_hbm.at[at], w.at[at], sems.at[i]))
        loads[i].start()

    def clear(i, carry):
        acc[i] = jnp.zeros((BLK, BLK), f32)
        return carry

    lax.fori_loop(0, SLOTS, clear, 0)
    for x in loads:
        x.wait()
    products(plan, 0, w, src, acc)


acc_shape = jax.ShapeDtypeStruct((SLOTS, BLK, BLK), f32)


def call_first(plan, w, src):
    return pl.pallas_call(
        first_kernel,
        out_shape=[acc_shape, blocks(WB)],
        in_specs=[sm_spec, any_spec, vm_spec],
        out_specs=[vm_spec, vm_spec],
        scratch_shapes=[pltpu.SemaphoreType.DMA((CHUNKS,))],
        name="own",
        compiler_params=limit(24),
        cost_estimate=cost(2_000_000_000),
    )(plan, w, src)


def more_kernel(classes, plan, w, *refs):
    acc = refs[-1]
    for cls, tab in zip(classes, refs):
        products(plan, cls, w, tab, acc)


def call_more(classes, plan, w, tables, acc):
    return pl.pallas_call(
        functools.partial(more_kernel, classes),
        out_shape=acc_shape,
        in_specs=[sm_spec] + [vm_spec] * (2 + len(tables)),
        out_specs=vm_spec,
        input_output_aliases={2 + len(tables): 0},
        compiler_params=limit(VLIM),
        cost_estimate=cost(1_000_000_000),
    )(plan, w, *tables, acc)


def exchange_kernel(n, ny, acc, got, qbuf, send_sem, recv_sem):
    me = lax.axis_index(AXES)
    side = 1 - 2 * (me % 2)
    barrier = pltpu.get_barrier_semaphore()
    peers = [me + 2 * side, me - 2 * side, me - side, me + side]
    valid = [(p >= 0) & (p < n) for p in peers]
    count = 0
    for p, ok in zip(peers, valid):
        count = count + ok.astype(i32)

        @pl.when(ok)
        def _(p=p):
            pl.semaphore_signal(barrier, inc=1, device_id=(p // ny, p % ny), device_id_type=pl.DeviceIdType.MESH)

    half = CT // 2
    slots = (1, 2, 4, 3)
    comes = [valid[1], valid[0], valid[2], valid[3]]

    def quantize(c):
        f, h = c // 2, c % 2

        def four(g, carry):
            for u in range(4):
                s = g * 4 + u
                x = acc[slots[f] * CT + h * half + s]
                top = jnp.max(jnp.abs(x), axis=0, keepdims=True)
                e = jnp.ceil(jnp.log2(jnp.maximum(top, 1e-30)))
                q = jnp.clip(jnp.round(x * jnp.exp2(15.0 - e)), -32767.0, 32767.0)
                row = pl.multiple_of(s * BLK, BLK)
                qbuf[c, pl.ds(row, BLK), :] = q.astype(i32).astype(jnp.int16)
                carry = jnp.where(lax.broadcasted_iota(i32, (16, BLK), 0) == s, e.astype(i32), carry)
            return carry

        exps = lax.fori_loop(0, half // 4, four, jnp.zeros((16, BLK), i32))
        qbuf[c, pl.ds(half * BLK, 16), :] = exps.astype(jnp.int16)

    def copy(c):
        p = peers[c // 2]
        return pltpu.make_async_remote_copy(
            src_ref=qbuf.at[c],
            dst_ref=got.at[c],
            send_sem=send_sem.at[c],
            recv_sem=recv_sem.at[c],
            device_id=(p // ny, p % ny),
            device_id_type=pl.DeviceIdType.MESH,
        )

    def send(c):
        @pl.when(valid[c // 2])
        def _():
            copy(c).start()

    quantize(0)
    quantize(1)
    pl.semaphore_wait(barrier, count)
    for c in range(1, 8):
        if c > 1:
            quantize(c)
        send(c - 1)
    send(7)

    for c in range(8):

        @pl.when(valid[c // 2])
        def _(c=c):
            copy(c).wait_send()

        @pl.when(comes[c // 2])
        def _(c=c):
            copy(c).wait_recv()


def call_exchange(n, ny, acc):
    shape = (8, HALF_ROWS, BLK)
    return pl.pallas_call(
        functools.partial(exchange_kernel, n, ny),
        out_shape=jax.ShapeDtypeStruct(shape, jnp.int16),
        in_specs=[vm_spec],
        out_specs=vm_spec,
        scratch_shapes=[
            pltpu.VMEM(shape, jnp.int16),
            pltpu.SemaphoreType.DMA((8,)),
            pltpu.SemaphoreType.DMA((8,)),
        ],
        name="exchange",
        compiler_params=pltpu.CompilerParams(vmem_limit_bytes=VLIM * 1024 * 1024, collective_id=0, has_side_effects=True),
        cost_estimate=cost(1_000_000_000),
    )(acc)


def final_kernel(recv, own, got, out, total, stage, sems):
    def clear(i, carry):
        total[i] = jnp.zeros((BLK, BLK), f32)
        return carry

    lax.fori_loop(0, TB, clear, 0)

    def add_own(r, carry):
        total[recv[0, r]] = own[r]
        return carry

    lax.fori_loop(0, CT, add_own, 0)
    half = CT // 2
    for c in range(8):
        scale = jnp.exp2(got[c, pl.ds(half * BLK, 16), :].astype(f32) - 15.0)
        for r in range(half):
            t = recv[(1, 2, 4, 3)[c // 2], (c % 2) * half + r]
            total[t] = total[t] + got[c, pl.ds(r * BLK, BLK), :].astype(f32) * scale[r : r + 1, :]
    step = TB // 4
    writes = []
    for j in range(4):

        def store(i, carry):
            stage[i] = total[i].astype(bf16)
            return carry

        lax.fori_loop(j * step, (j + 1) * step, store, 0)
        at = pl.ds(j * step, step)
        writes.append(pltpu.make_async_copy(stage.at[at], out.at[at], sems.at[j]))
        if j:
            writes[j - 1].start()
    writes[3].start()
    for x in writes:
        x.wait()


def call_final(recv, own, got):
    return pl.pallas_call(
        final_kernel,
        out_shape=jax.ShapeDtypeStruct((TB, BLK, BLK), bf16),
        in_specs=[sm_spec, vm_spec, vm_spec],
        out_specs=any_spec,
        scratch_shapes=[
            pltpu.VMEM((TB + 1, BLK, BLK), f32),
            pltpu.VMEM((TB, BLK, BLK), bf16),
            pltpu.SemaphoreType.DMA((4,)),
        ],
        name="final",
        compiler_params=limit(VLIM),
        cost_estimate=cost(100_000_000),
    )(recv, own, got)


def swaps(n):
    def pairs(step):
        moves = [(d, d + step * (1 - 2 * (d % 2))) for d in range(n)]
        return [(d, t) for d, t in moves if 0 <= t < n]

    return pairs(2), pairs(-2), pairs(-1), pairs(1)


def remap(source_field, weight_blocks, source_ids, target_ids):
    n = lax.axis_size(AXES)
    out_two, in_two, across, partner = swaps(n)
    sids = source_ids.reshape(n, 4, BLK)
    tids = target_ids.reshape(n, 4, BLK)
    send = lambda x, pairs: lax.ppermute(x, AXES, pairs)
    pn = call_union(n, sids, source_field)
    got_n = send(pn, across)
    py, px, pz, pd, pt, plan, recv = call_plan(n, sids, tids, source_field)
    got_y = send(py, in_two)
    got_d = send(pd, partner)
    over = call_excess(sids)[0, 0] > 0
    tail_n, tail_y = lax.cond(
        over,
        lambda t: (send(t, across), send(t, in_two)),
        lambda t: (jnp.zeros_like(t), jnp.zeros_like(t)),
        pt,
    )
    plan, tail_n, tail_y = lax.optimization_barrier((plan, tail_n, tail_y))
    acc, w = call_first(plan, weight_blocks, source_field)
    px, pz, acc = lax.optimization_barrier((px, pz, acc))
    got_x = send(px, out_two)
    got_z = send(pz, out_two)
    swap_n = send(got_n, partner)
    acc = call_more((3, 1, 2), plan, w, (got_d, got_n, swap_n), acc)
    acc, got_y = lax.optimization_barrier((acc, got_y))
    swap_y = send(got_y, partner)
    acc = call_more((4, 5, 7, 8), plan, w, (got_y, swap_y, tail_n, tail_y), acc)
    acc = call_more((6,), plan, w, (got_x,), acc)
    acc = call_more((9,), plan, w, (got_z,), acc)
    got = call_exchange(n, lax.axis_size("gy"), acc)
    return call_final(recv, acc, got)


def solution(mesh):
    return jax.shard_map(
        remap,
        mesh=mesh,
        in_specs=(P(AXES, None, None), P(AXES, None, None), P(), P()),
        out_specs=P(AXES, None, None),
        check_vma=False,
    )
```

profile of v0, /device:TPU:8, one launch (start us, length us, event | category | flops | bytes accessed | tf_op | source)
XLA Modules:
  0.0 124.4 jit_solution(318757718354961657)
XLA Ops:
  0.0 3.6 %union.1 = bf16[54,128,128]{2,1,0:T(8,128)(2,1)} custom-call(s32[128,4,128]{2,1,0:T(4,128)} %bitcast.3, bf16[128,128,128]{2,1,0:T(8,128)(2,1)} %src.3), custom_call_target="tpu_custom_call" | custom-call | flops 1000000 | bytes 8000000 | tf_op jit(solution)/shard_map/union/pallas_call | solution.py:269
  3.6 7.5 %collective-permute-start.5 = (bf16[54,128,128]{2,1,0:T(8,128)(2,1)}, bf16[54,128,128]{2,1,0:T(8,128)(2,1)}, u32[]{:S(2)}, u32[]{:S(2)}) collective-permute-start(bf16[54,128,128]{2,1,0:T(8,128)(2,1)} %union.1), channel_id=1, source_target_pairs={{1,2},{2,1},{3,4},{4,3},{5,6},{6,5},{7,8},{8,7},{9,10},{10,9},{11,... | collective-permute-start | bytes 5308424 | tf_op jit(solution)/shard_map/ppermute | solution.py:538
  11.1 2.2 %copy-done = bf16[128,128,128]{2,1,0:T(8,128)(2,1)S(1)} copy-done((bf16[128,128,128]{2,1,0:T(8,128)(2,1)S(1)}, bf16[128,128,128]{2,1,0:T(8,128)(2,1)}, u32[]{:S(2)}) %copy-start) | copy-done | bytes 4194328
  13.3 5.5 %plan.1 = (bf16[52,128,128]{2,1,0:T(8,128)(2,1)}, bf16[44,128,128]{2,1,0:T(8,128)(2,1)S(1)}, bf16[20,128,128]{2,1,0:T(8,128)(2,1)S(1)}, bf16[64,128,128]{2,1,0:T...) custom-call(s32[128,4,128]{2,1,0:T(4,128)S(1)} %bitcast.4, ...), custom_call_target="tpu_custom_call" | custom-call | flops 500000000 | bytes 8000000 | tf_op jit(solution)/shard_map/plan/pallas_call | solution.py:288
  18.8 0.1 collective-permute-start.4
  18.9 13.1 %collective-permute-done.5.refs_1_ = bf16[54,128,128]{2,1,0:T(8,128)(2,1)} collective-permute-done((bf16[54,128,128]{2,1,0:T(8,128)(2,1)}, bf16[54,128,128]{2,1,0:T(8,128)(2,1)}, u32[]{:S(2)}, u32[]{:S(2)}) %collective-permute-start.5) | collective-permute-done | bytes 1769504 | tf_op jit(solution)/shard_map/ppermute | solution.py:538
  32.0 7.8 %collective-permute-start.7 = (bf16[52,128,128]{2,1,0:T(8,128)(2,1)}, bf16[52,128,128]{2,1,0:T(8,128)(2,1)}, u32[]{:S(2)}, u32[]{:S(2)}) collective-permute-start(bf16[52,128,128]{2,1,0:T(8,128)(2,1)} %get-tuple-element.39), channel_id=1, source_target_pairs={{1,3},{2,0},{3,5},{4,2},{5,7},{6,4},{7,9},{8,6},{9,11},{10,8},{11,... | collective-permute-start | bytes 5111816 | tf_op jit(solution)/shard_map/ppermute | solution.py:538
  39.8 0.6 excess.1
  40.5 0.5 slice.3
  41.6 2.1 %conditional.1 = (bf16[22,128,128]{2,1,0:T(8,128)(2,1)}, bf16[22,128,128]{2,1,0:T(8,128)(2,1)}) conditional(s32[]{:T(128)} %bitcast.2, () %tuple.16, bf16[22,128,128]{2,1,0:T(8,128)(2,1)S(1)} %get-tuple-element.27), branch_computations={%region_0.0_spmd, %region_1.0_spmd} | conditional | bytes 5767264 | solution.py:545
  41.7 1.0 broadcast.2.clone
  42.7 1.1 broadcast.2
  43.8 2.2 %copy-done.1 = bf16[128,128,128]{2,1,0:T(8,128)(2,1)S(1)} copy-done((bf16[128,128,128]{2,1,0:T(8,128)(2,1)S(1)}, bf16[128,128,128]{2,1,0:T(8,128)(2,1)}, u32[]{:S(2)}) %copy-start.1) | copy-done | bytes 4194328
  45.9 10.2 %own.1 = (f32[84,128,128]{2,1,0:T(8,128)S(1)}, bf16[512,128,128]{2,1,0:T(8,128)(2,1)S(1)}) custom-call(s32[8,128]{1,0:T(8,128)S(1)} %get-tuple-element.30.plan, bf16[512,128,128]{2,1,0:T(8,128)(2,1)} %w_hbm.1, bf16[128,128,128]{2,1,0:T(8,128)(2,1)S(1)} %copy-done.1), custom_call_target="tpu_custom_call" | custom-call | flops 2000000000 | bytes 8000000 | tf_op jit(solution)/shard_map/own/pallas_call | solution.py:352
  56.2 6.5 %shard_map.46.refs_4_ = f32[84,128,128]{2,1,0:T(8,128)S(1)} custom-call(s32[8,128]{1,0:T(8,128)S(1)} %get-tuple-element.30.plan, bf16[512,128,128]{2,1,0:T(8,128)(2,1)S(1)} %get-tuple-element.31.w, bf16[64,128,128]{2,1,0:T(8,128)(2,1)S(1)} %collective-permute-done.4.refs_0_, ...), custom_call_target="tpu_custom_call", output_to_operand_aliasing={{}: (5, {})} | custom-call | flops 1000000000 | bytes 8000000 | tf_op jit(solution)/shard_map/pallas_call | solution.py:371
  62.8 1.9 %collective-permute-start.3 = (bf16[44,128,128]{2,1,0:T(8,128)(2,1)S(1)}, bf16[44,128,128]{2,1,0:T(8,128)(2,1)S(1)}, u32[]{:S(2)}, u32[]{:S(2)}) collective-permute-start(bf16[44,128,128]{2,1,0:T(8,128)(2,1)S(1)} %copy-done.5), channel_id=1, source_target_pairs={{0,2},{2,4},{3,1},{4,6},{5,3},{6,8},{7,5},{8,10},{9,7},{10,12},{11... | collective-permute-start | bytes 4325384 | tf_op jit(solution)/shard_map/ppermute | solution.py:538
  64.7 1.9 %collective-permute-start.2 = (bf16[20,128,128]{2,1,0:T(8,128)(2,1)S(1)}, bf16[20,128,128]{2,1,0:T(8,128)(2,1)S(1)}, u32[]{:S(2)}, u32[]{:S(2)}) collective-permute-start(bf16[20,128,128]{2,1,0:T(8,128)(2,1)S(1)} %get-tuple-element.35), channel_id=1, source_target_pairs={{0,2},{2,4},{3,1},{4,6},{5,3},{6,8},{7,5},{8,10},{9,7},{10,12},{11... | collective-permute-start | bytes 1966088 | tf_op jit(solution)/shard_map/ppermute | solution.py:538
  66.6 2.8 %shard_map.47.refs_1_ = f32[84,128,128]{2,1,0:T(8,128)S(1)} custom-call(s32[8,128]{1,0:T(8,128)S(1)} %get-tuple-element.30.plan, bf16[512,128,128]{2,1,0:T(8,128)(2,1)S(1)} %get-tuple-element.31.w, bf16[52,128,128]{2,1,0:T(8,128)(2,1)} %collective-permute-done.7.refs_0_, ...), custom_call_target="tpu_custom_call", output_to_operand_aliasing={{}: (6, {})} | custom-call | flops 1000000000 | bytes 8000000 | tf_op jit(solution)/shard_map/pallas_call | solution.py:371
  69.5 18.4 %collective-permute-done.3.refs_0_ = bf16[44,128,128]{2,1,0:T(8,128)(2,1)S(1)} collective-permute-done((bf16[44,128,128]{2,1,0:T(8,128)(2,1)S(1)}, bf16[44,128,128]{2,1,0:T(8,128)(2,1)S(1)}, u32[]{:S(2)}, u32[]{:S(2)}) %collective-permute-start.3) | collective-permute-done | bytes 1441824 | tf_op jit(solution)/shard_map/ppermute | solution.py:538
  87.9 2.1 %shard_map.48.refs_1_ = f32[84,128,128]{2,1,0:T(8,128)S(1)} custom-call(s32[8,128]{1,0:T(8,128)S(1)} %get-tuple-element.30.plan, bf16[512,128,128]{2,1,0:T(8,128)(2,1)S(1)} %get-tuple-element.31.w, bf16[44,128,128]{2,1,0:T(8,128)(2,1)S(1)} %collective-permute-done.3.refs_0_, f32[84,128,128]{2,1,0:T(8,128)S(1)} %shard_map.47.refs_1_), custom_call_target="tpu_custom_call", output_to_operand_aliasing={{}: (3, {})} | custom-call | flops 1000000000 | bytes 8000000 | tf_op jit(solution)/shard_map/pallas_call | solution.py:371
  90.0 4.9 %collective-permute-done.2.refs_0_ = bf16[20,128,128]{2,1,0:T(8,128)(2,1)S(1)} collective-permute-done((bf16[20,128,128]{2,1,0:T(8,128)(2,1)S(1)}, bf16[20,128,128]{2,1,0:T(8,128)(2,1)S(1)}, u32[]{:S(2)}, u32[]{:S(2)}) %collective-permute-start.2) | collective-permute-done | bytes 655392 | tf_op jit(solution)/shard_map/ppermute | solution.py:538
  94.9 1.2 shard_map.49.acc.own
  96.1 24.9 %exchange.1.got = s16[8,1040,128]{2,1,0:T(8,128)(2,1)S(1)} custom-call(f32[84,128,128]{2,1,0:T(8,128)S(1)} %shard_map.49.acc.own), custom_call_target="tpu_custom_call" | custom-call | flops 1000000000 | bytes 8000000 | tf_op jit(solution)/shard_map/exchange/pallas_call | solution.py:456
  121.0 3.3 %final.1 = bf16[64,128,128]{2,1,0:T(8,128)(2,1)} custom-call(s32[8,128]{1,0:T(8,128)S(1)} %get-tuple-element.25.recv, f32[84,128,128]{2,1,0:T(8,128)S(1)} %shard_map.49.acc.own, s16[8,1040,128]{2,1,0:T(8,128)(2,1)S(1)} %exchange.1.got), custom_call_target="tpu_custom_call" | custom-call | flops 100000000 | bytes 8000000 | tf_op jit(solution)/shard_map/final/pallas_call | solution.py:509
  (16 shorter events, 0.1 us)
Async XLA Ops:
  0.0 11.1 %copy-start.2 = (s32[65536]{0:T(1024)S(1)}, s32[65536]{0:T(1024)}, u32[]{:S(2)}) copy-start(s32[65536]{0:T(1024)} %param.8) | copy-start | bytes 786436
  0.0 11.1 %copy-start.3 = (s32[65536]{0:T(1024)S(1)}, s32[65536]{0:T(1024)}, u32[]{:S(2)}) copy-start(s32[65536]{0:T(1024)} %param.9) | copy-start | bytes 786436
  3.6 28.4 %collective-permute-start.5 = (bf16[54,128,128]{2,1,0:T(8,128)(2,1)}, bf16[54,128,128]{2,1,0:T(8,128)(2,1)}, u32[]{:S(2)}, u32[]{:S(2)}) collective-permute-start(bf16[54,128,128]{2,1,0:T(8,128)(2,1)} %union.1), channel_id=1, source_target_pairs={{1,2},{2,1},{3,4},{4,3},{5,6},{6,5},{7,8},{8,7},{9,10},{10,9},{11,... | collective-permute-start | bytes 5308424 | tf_op jit(solution)/shard_map/ppermute | solution.py:538
  11.1 2.2 %copy-start = (bf16[128,128,128]{2,1,0:T(8,128)(2,1)S(1)}, bf16[128,128,128]{2,1,0:T(8,128)(2,1)}, u32[]{:S(2)}) copy-start(bf16[128,128,128]{2,1,0:T(8,128)(2,1)} %src.3) | copy-start | bytes 12582916
  18.8 21.7 %copy-start.4 = (bf16[44,128,128]{2,1,0:T(8,128)(2,1)}, bf16[44,128,128]{2,1,0:T(8,128)(2,1)S(1)}, u32[]{:S(2)}) copy-start(bf16[44,128,128]{2,1,0:T(8,128)(2,1)S(1)} %get-tuple-element.36) | copy-start | bytes 4325380
  18.8 37.3 %collective-permute-start.4 = (bf16[64,128,128]{2,1,0:T(8,128)(2,1)}, bf16[64,128,128]{2,1,0:T(8,128)(2,1)S(1)}, u32[]{:S(2)}, u32[]{:S(2)}) collective-permute-start(bf16[64,128,128]{2,1,0:T(8,128)(2,1)} %get-tuple-element.37), channel_id=1, source_target_pairs={{0,1},{1,0},{2,3},{3,2},{4,5},{5,4},{6,7},{7,6},{8,9},{9,8},{10,11... | collective-permute-start | bytes 6291464 | tf_op jit(solution)/shard_map/ppermute | solution.py:538
  32.0 24.2 %collective-permute-start.6 = (bf16[54,128,128]{2,1,0:T(8,128)(2,1)}, bf16[54,128,128]{2,1,0:T(8,128)(2,1)}, u32[]{:S(2)}, u32[]{:S(2)}) collective-permute-start(bf16[54,128,128]{2,1,0:T(8,128)(2,1)} %collective-permute-done.5.refs_1_), channel_id=1, source_target_pairs={{0,1},{1,0},{2,3},{3,2},{4,5},{5,4},{6,7},{7,6},{8,9},{9,8},{10,11... | collective-permute-start | bytes 5308424 | tf_op jit(solution)/shard_map/ppermute | solution.py:538
  32.0 30.7 %collective-permute-start.7 = (bf16[52,128,128]{2,1,0:T(8,128)(2,1)}, bf16[52,128,128]{2,1,0:T(8,128)(2,1)}, u32[]{:S(2)}, u32[]{:S(2)}) collective-permute-start(bf16[52,128,128]{2,1,0:T(8,128)(2,1)} %get-tuple-element.39), channel_id=1, source_target_pairs={{1,3},{2,0},{3,5},{4,2},{5,7},{6,4},{7,9},{8,6},{9,11},{10,8},{11,... | collective-permute-start | bytes 5111816 | tf_op jit(solution)/shard_map/ppermute | solution.py:538
  43.8 2.2 %copy-start.1 = (bf16[128,128,128]{2,1,0:T(8,128)(2,1)S(1)}, bf16[128,128,128]{2,1,0:T(8,128)(2,1)}, u32[]{:S(2)}) copy-start(bf16[128,128,128]{2,1,0:T(8,128)(2,1)} %src.3) | copy-start | bytes 12582916
  56.2 6.6 %copy-start.5 = (bf16[44,128,128]{2,1,0:T(8,128)(2,1)S(1)}, bf16[44,128,128]{2,1,0:T(8,128)(2,1)}, u32[]{:S(2)}) copy-start(bf16[44,128,128]{2,1,0:T(8,128)(2,1)} %copy-done.4) | copy-start | bytes 4325380
  62.7 4.0 %collective-permute-start.8 = (bf16[52,128,128]{2,1,0:T(8,128)(2,1)}, bf16[52,128,128]{2,1,0:T(8,128)(2,1)S(1)}, u32[]{:S(2)}, u32[]{:S(2)}) collective-permute-start(bf16[52,128,128]{2,1,0:T(8,128)(2,1)} %collective-permute-done.7.refs_0_), channel_id=1, source_target_pairs={{0,1},{1,0},{2,3},{3,2},{4,5},{5,4},{6,7},{7,6},{8,9},{9,8},{10,11... | collective-permute-start | bytes 5111816 | tf_op jit(solution)/shard_map/ppermute | solution.py:538
  62.8 25.1 %collective-permute-start.3 = (bf16[44,128,128]{2,1,0:T(8,128)(2,1)S(1)}, bf16[44,128,128]{2,1,0:T(8,128)(2,1)S(1)}, u32[]{:S(2)}, u32[]{:S(2)}) collective-permute-start(bf16[44,128,128]{2,1,0:T(8,128)(2,1)S(1)} %copy-done.5), channel_id=1, source_target_pairs={{0,2},{2,4},{3,1},{4,6},{5,3},{6,8},{7,5},{8,10},{9,7},{10,12},{11... | collective-permute-start | bytes 4325384 | tf_op jit(solution)/shard_map/ppermute | solution.py:538
  64.7 30.2 %collective-permute-start.2 = (bf16[20,128,128]{2,1,0:T(8,128)(2,1)S(1)}, bf16[20,128,128]{2,1,0:T(8,128)(2,1)S(1)}, u32[]{:S(2)}, u32[]{:S(2)}) collective-permute-start(bf16[20,128,128]{2,1,0:T(8,128)(2,1)S(1)} %get-tuple-element.35), channel_id=1, source_target_pairs={{0,2},{2,4},{3,1},{4,6},{5,3},{6,8},{7,5},{8,10},{9,7},{10,12},{11... | collective-permute-start | bytes 1966088 | tf_op jit(solution)/shard_map/ppermute | solution.py:538
where the time goes:
time: 125 us; the launch traced here: 124 us
  Pallas kernels  60.8 us (49%)
  waiting for transfers between devices  36.4 us (29%)
  starting transfers between devices  19.3 us (15%)
  local copies, waits for them, and re-layouts  7.02 us (6%)
    ppermute x7, waiting for transfers between devices, remap(): send = lambda x, pairs: lax.ppermute(x, AXES, pairs)  36.4 us
    pallas_call x1, Pallas kernels, call_exchange(): pl.pallas_call(functools.partial(exchange_kernel, n, ny), out_shape=jax.S...  24.9 us
    ppermute x7, starting transfers between devices, remap(): send = lambda x, pairs: lax.ppermute(x, AXES, pairs)  19.3 us
    pallas_call x4, Pallas kernels, call_more(): pl.pallas_call(functools.partial(more_kernel, classes), out_shape=acc_sha...  12.6 us
    pallas_call x1, Pallas kernels, call_first(): pl.pallas_call(first_kernel, out_shape=[acc_shape, blocks(WB)], in_specs=...  10.2 us
    pallas_call x1, Pallas kernels, call_plan(): pl.pallas_call(functools.partial(plan_kernel, n), out_shape=[blocks(c) fo...  5.53 us
    unnamed x12, local copies, waits for them, and re-layouts  4.39 us
    pallas_call x1, Pallas kernels, call_union(): pl.pallas_call(functools.partial(union_kernel, n), out_shape=blocks(PART)...  3.6 us
  transfers between devices with their start and end apart: 7, of which 3 were waited for; matrix products, arithmetic and copies ran while one was open for 2% of the time, Pallas kernels for 22%

commit v1 on v0

--- a/solution.py
+++ b/solution.py
@@ -18,11 +18,10 @@
 TRASH = 80
 SLOTS = 84
 GROUP = 16
-PART = 54
-PART_B = 52
-UNION = PART + PART_B
+PART = 52
+UNION = 2 * PART
 TAIL = SB - UNION
-FAR = 44
+FAR = 52
 REST = CS - FAR
 HEADS = 6
 VLIM = 9
@@ -114,12 +113,12 @@
     fetch.wait()
 
     def send(r, carry):
-        for u in range(6):
-            b = list_s[0, r * 6 + u]
-            pltpu.make_async_copy(src_v.at[b], pn.at[r * 6 + u], sems.at[2]).start()
+        for u in range(4):
+            b = list_s[0, r * 4 + u]
+            pltpu.make_async_copy(src_v.at[b], pn.at[r * 4 + u], sems.at[2]).start()
         return carry
 
-    lax.fori_loop(0, PART // 6, send, 0)
+    lax.fori_loop(0, PART // 4, send, 0)
     pltpu.make_async_copy(src_v.at[pl.ds(0, PART)], pn, sems.at[2]).wait()
 
 
@@ -202,7 +201,7 @@
         recv[f : f + 1, :] = listed(present, ranks(present), float(TB))
 
     move.wait()
-    pack(src_v, list_s, 2, PART, py, PART_B)
+    pack(src_v, list_s, 2, PART, py, PART)
     pack(src_v, list_s, 0, 0, px, FAR)
     pack(src_v, list_s, 0, FAR, pz, REST)
     pack(src_v, list_s, 1, 0, pd, CS)
@@ -287,7 +286,7 @@
     table = jax.ShapeDtypeStruct((8, BLK), i32)
     return pl.pallas_call(
         functools.partial(plan_kernel, n),
-        out_shape=[blocks(c) for c in (PART_B, FAR, REST, CS, TAIL)] + [table] * 2,
+        out_shape=[blocks(c) for c in (PART, FAR, REST, CS, TAIL)] + [table] * 2,
         in_specs=[any_spec, any_spec, vm_spec],
         out_specs=[vm_spec] * 7,
         scratch_shapes=index_scratch(*[pltpu.VMEM((5, 4, BLK), i32)] * 2),

time: 125 us -> 124 us (level)
  the two profiles are of different devices: /device:TPU:8 before, /device:TPU:24 now
where the time goes in v1:
time: 124 us
  Pallas kernels  61.2 us (49%)
  waiting for transfers between devices  34.7 us (28%)
  starting transfers between devices  19.9 us (16%)
  local copies, waits for them, and re-layouts  7.16 us (6%)
    ppermute x7, waiting for transfers between devices, remap(): send = lambda x, pairs: lax.ppermute(x, AXES, pairs)  34.7 us
    pallas_call x1, Pallas kernels, call_exchange(): pl.pallas_call(functools.partial(exchange_kernel, n, ny), out_shape=jax.S...  24.9 us
    ppermute x7, starting transfers between devices, remap(): send = lambda x, pairs: lax.ppermute(x, AXES, pairs)  19.9 us
    pallas_call x4, Pallas kernels, call_more(): pl.pallas_call(functools.partial(more_kernel, classes), out_shape=acc_sha...  13 us
    pallas_call x1, Pallas kernels, call_first(): pl.pallas_call(first_kernel, out_shape=[acc_shape, blocks(WB)], in_specs=...  10.2 us
    pallas_call x1, Pallas kernels, call_plan(): pl.pallas_call(functools.partial(plan_kernel, n), out_shape=[blocks(c) fo...  5.54 us
    unnamed x12, local copies, waits for them, and re-layouts  4.39 us
    pallas_call x1, Pallas kernels, call_union(): pl.pallas_call(functools.partial(union_kernel, n), out_shape=blocks(PART)...  3.61 us
  transfers between devices with their start and end apart: 7, of which 3 were waited for; matrix products, arithmetic and copies ran while one was open for 2% of the time, Pallas kernels for 23%

profile of v1, /device:TPU:24, one launch (start us, length us, event | category | flops | bytes accessed | tf_op | source)
XLA Modules:
  0.0 123.8 jit_solution(5414759606940713473)
XLA Ops:
  0.0 3.6 %union.1 = bf16[52,128,128]{2,1,0:T(8,128)(2,1)} custom-call(s32[128,4,128]{2,1,0:T(4,128)} %bitcast.3, bf16[128,128,128]{2,1,0:T(8,128)(2,1)} %src.3), custom_call_target="tpu_custom_call" | custom-call | flops 1000000 | bytes 8000000 | tf_op jit(solution)/shard_map/union/pallas_call | solution.py:268
  3.6 7.8 %collective-permute-start.5 = (bf16[52,128,128]{2,1,0:T(8,128)(2,1)}, bf16[52,128,128]{2,1,0:T(8,128)(2,1)}, u32[]{:S(2)}, u32[]{:S(2)}) collective-permute-start(bf16[52,128,128]{2,1,0:T(8,128)(2,1)} %union.1), channel_id=1, source_target_pairs={{1,2},{2,1},{3,4},{4,3},{5,6},{6,5},{7,8},{8,7},{9,10},{10,9},{11,... | collective-permute-start | bytes 5111816 | tf_op jit(solution)/shard_map/ppermute | solution.py:537
  11.4 2.2 %copy-done = bf16[128,128,128]{2,1,0:T(8,128)(2,1)S(1)} copy-done((bf16[128,128,128]{2,1,0:T(8,128)(2,1)S(1)}, bf16[128,128,128]{2,1,0:T(8,128)(2,1)}, u32[]{:S(2)}) %copy-start) | copy-done | bytes 4194328
  13.6 5.5 %plan.1 = (bf16[52,128,128]{2,1,0:T(8,128)(2,1)}, bf16[52,128,128]{2,1,0:T(8,128)(2,1)S(1)}, bf16[12,128,128]{2,1,0:T(8,128)(2,1)S(1)}, bf16[64,128,128]{2,1,0:T...) custom-call(s32[128,4,128]{2,1,0:T(4,128)S(1)} %bitcast.4, ...), custom_call_target="tpu_custom_call" | custom-call | flops 500000000 | bytes 8000000 | tf_op jit(solution)/shard_map/plan/pallas_call | solution.py:287
  19.2 0.1 collective-permute-start.4
  19.2 12.0 %collective-permute-done.5.refs_1_ = bf16[52,128,128]{2,1,0:T(8,128)(2,1)} collective-permute-done((bf16[52,128,128]{2,1,0:T(8,128)(2,1)}, bf16[52,128,128]{2,1,0:T(8,128)(2,1)}, u32[]{:S(2)}, u32[]{:S(2)}) %collective-permute-start.5) | collective-permute-done | bytes 1703968 | tf_op jit(solution)/shard_map/ppermute | solution.py:537
  31.3 8.1 %collective-permute-start.7 = (bf16[52,128,128]{2,1,0:T(8,128)(2,1)}, bf16[52,128,128]{2,1,0:T(8,128)(2,1)}, u32[]{:S(2)}, u32[]{:S(2)}) collective-permute-start(bf16[52,128,128]{2,1,0:T(8,128)(2,1)} %get-tuple-element.39), channel_id=1, source_target_pairs={{1,3},{2,0},{3,5},{4,2},{5,7},{6,4},{7,9},{8,6},{9,11},{10,8},{11,... | collective-permute-start | bytes 5111816 | tf_op jit(solution)/shard_map/ppermute | solution.py:537
  39.4 0.6 excess.1
  40.1 0.6 slice.3
  41.3 2.2 %conditional.1 = (bf16[24,128,128]{2,1,0:T(8,128)(2,1)}, bf16[24,128,128]{2,1,0:T(8,128)(2,1)}) conditional(s32[]{:T(128)} %bitcast.2, () %tuple.16, bf16[24,128,128]{2,1,0:T(8,128)(2,1)S(1)} %get-tuple-element.27), branch_computations={%region_0.0_spmd, %region_1.0_spmd} | conditional | bytes 6291552 | solution.py:544
  41.3 1.0 broadcast.2.clone
  42.4 1.1 broadcast.2
  43.5 2.2 %copy-done.1 = bf16[128,128,128]{2,1,0:T(8,128)(2,1)S(1)} copy-done((bf16[128,128,128]{2,1,0:T(8,128)(2,1)S(1)}, bf16[128,128,128]{2,1,0:T(8,128)(2,1)}, u32[]{:S(2)}) %copy-start.1) | copy-done | bytes 4194328
  45.7 10.2 %own.1 = (f32[84,128,128]{2,1,0:T(8,128)S(1)}, bf16[512,128,128]{2,1,0:T(8,128)(2,1)S(1)}) custom-call(s32[8,128]{1,0:T(8,128)S(1)} %get-tuple-element.30.plan, bf16[512,128,128]{2,1,0:T(8,128)(2,1)} %w_hbm.1, bf16[128,128,128]{2,1,0:T(8,128)(2,1)S(1)} %copy-done.1), custom_call_target="tpu_custom_call" | custom-call | flops 2000000000 | bytes 8000000 | tf_op jit(solution)/shard_map/own/pallas_call | solution.py:351
  55.9 6.1 %shard_map.46.refs_4_ = f32[84,128,128]{2,1,0:T(8,128)S(1)} custom-call(s32[8,128]{1,0:T(8,128)S(1)} %get-tuple-element.30.plan, bf16[512,128,128]{2,1,0:T(8,128)(2,1)S(1)} %get-tuple-element.31.w, bf16[64,128,128]{2,1,0:T(8,128)(2,1)S(1)} %collective-permute-done.4.refs_0_, ...), custom_call_target="tpu_custom_call", output_to_operand_aliasing={{}: (5, {})} | custom-call | flops 1000000000 | bytes 8000000 | tf_op jit(solution)/shard_map/pallas_call | solution.py:370
  62.2 1.9 %collective-permute-start.3 = (bf16[52,128,128]{2,1,0:T(8,128)(2,1)S(1)}, bf16[52,128,128]{2,1,0:T(8,128)(2,1)S(1)}, u32[]{:S(2)}, u32[]{:S(2)}) collective-permute-start(bf16[52,128,128]{2,1,0:T(8,128)(2,1)S(1)} %copy-done.5), channel_id=1, source_target_pairs={{0,2},{2,4},{3,1},{4,6},{5,3},{6,8},{7,5},{8,10},{9,7},{10,12},{11... | collective-permute-start | bytes 5111816 | tf_op jit(solution)/shard_map/ppermute | solution.py:537
  64.1 1.9 %collective-permute-start.2 = (bf16[12,128,128]{2,1,0:T(8,128)(2,1)S(1)}, bf16[12,128,128]{2,1,0:T(8,128)(2,1)S(1)}, u32[]{:S(2)}, u32[]{:S(2)}) collective-permute-start(bf16[12,128,128]{2,1,0:T(8,128)(2,1)S(1)} %get-tuple-element.35), channel_id=1, source_target_pairs={{0,2},{2,4},{3,1},{4,6},{5,3},{6,8},{7,5},{8,10},{9,7},{10,12},{11... | collective-permute-start | bytes 1179656 | tf_op jit(solution)/shard_map/ppermute | solution.py:537
  66.1 3.2 %shard_map.47.refs_1_ = f32[84,128,128]{2,1,0:T(8,128)S(1)} custom-call(s32[8,128]{1,0:T(8,128)S(1)} %get-tuple-element.30.plan, bf16[512,128,128]{2,1,0:T(8,128)(2,1)S(1)} %get-tuple-element.31.w, bf16[52,128,128]{2,1,0:T(8,128)(2,1)} %collective-permute-done.7.refs_0_, ...), custom_call_target="tpu_custom_call", output_to_operand_aliasing={{}: (6, {})} | custom-call | flops 1000000000 | bytes 8000000 | tf_op jit(solution)/shard_map/pallas_call | solution.py:370
  69.2 20.9 %collective-permute-done.3.refs_0_ = bf16[52,128,128]{2,1,0:T(8,128)(2,1)S(1)} collective-permute-done((bf16[52,128,128]{2,1,0:T(8,128)(2,1)S(1)}, bf16[52,128,128]{2,1,0:T(8,128)(2,1)S(1)}, u32[]{:S(2)}, u32[]{:S(2)}) %collective-permute-start.3) | collective-permute-done | bytes 1703968 | tf_op jit(solution)/shard_map/ppermute | solution.py:537
  90.1 2.5 %shard_map.48.refs_1_ = f32[84,128,128]{2,1,0:T(8,128)S(1)} custom-call(s32[8,128]{1,0:T(8,128)S(1)} %get-tuple-element.30.plan, bf16[512,128,128]{2,1,0:T(8,128)(2,1)S(1)} %get-tuple-element.31.w, bf16[52,128,128]{2,1,0:T(8,128)(2,1)S(1)} %collective-permute-done.3.refs_0_, f32[84,128,128]{2,1,0:T(8,128)S(1)} %shard_map.47.refs_1_), custom_call_target="tpu_custom_call", output_to_operand_aliasing={{}: (3, {})} | custom-call | flops 1000000000 | bytes 8000000 | tf_op jit(solution)/shard_map/pallas_call | solution.py:370
  92.6 1.7 %collective-permute-done.2.refs_0_ = bf16[12,128,128]{2,1,0:T(8,128)(2,1)S(1)} collective-permute-done((bf16[12,128,128]{2,1,0:T(8,128)(2,1)S(1)}, bf16[12,128,128]{2,1,0:T(8,128)(2,1)S(1)}, u32[]{:S(2)}, u32[]{:S(2)}) %collective-permute-start.2) | collective-permute-done | bytes 393248 | tf_op jit(solution)/shard_map/ppermute | solution.py:537
  94.3 1.2 shard_map.49.acc.own
  95.6 24.9 %exchange.1.got = s16[8,1040,128]{2,1,0:T(8,128)(2,1)S(1)} custom-call(f32[84,128,128]{2,1,0:T(8,128)S(1)} %shard_map.49.acc.own), custom_call_target="tpu_custom_call" | custom-call | flops 1000000000 | bytes 8000000 | tf_op jit(solution)/shard_map/exchange/pallas_call | solution.py:455
  120.5 3.3 %final.1 = bf16[64,128,128]{2,1,0:T(8,128)(2,1)} custom-call(s32[8,128]{1,0:T(8,128)S(1)} %get-tuple-element.25.recv, f32[84,128,128]{2,1,0:T(8,128)S(1)} %shard_map.49.acc.own, s16[8,1040,128]{2,1,0:T(8,128)(2,1)S(1)} %exchange.1.got), custom_call_target="tpu_custom_call" | custom-call | flops 100000000 | bytes 8000000 | tf_op jit(solution)/shard_map/final/pallas_call | solution.py:508
  (16 shorter events, 0.1 us)
Async XLA Ops:
  0.0 11.4 %copy-start.2 = (s32[65536]{0:T(1024)S(1)}, s32[65536]{0:T(1024)}, u32[]{:S(2)}) copy-start(s32[65536]{0:T(1024)} %param.8) | copy-start | bytes 786436
  0.0 11.4 %copy-start.3 = (s32[65536]{0:T(1024)S(1)}, s32[65536]{0:T(1024)}, u32[]{:S(2)}) copy-start(s32[65536]{0:T(1024)} %param.9) | copy-start | bytes 786436
  3.6 27.7 %collective-permute-start.5 = (bf16[52,128,128]{2,1,0:T(8,128)(2,1)}, bf16[52,128,128]{2,1,0:T(8,128)(2,1)}, u32[]{:S(2)}, u32[]{:S(2)}) collective-permute-start(bf16[52,128,128]{2,1,0:T(8,128)(2,1)} %union.1), channel_id=1, source_target_pairs={{1,2},{2,1},{3,4},{4,3},{5,6},{6,5},{7,8},{8,7},{9,10},{10,9},{11,... | collective-permute-start | bytes 5111816 | tf_op jit(solution)/shard_map/ppermute | solution.py:537
  11.4 2.2 %copy-start = (bf16[128,128,128]{2,1,0:T(8,128)(2,1)S(1)}, bf16[128,128,128]{2,1,0:T(8,128)(2,1)}, u32[]{:S(2)}) copy-start(bf16[128,128,128]{2,1,0:T(8,128)(2,1)} %src.3) | copy-start | bytes 12582916
  19.1 20.9 %copy-start.4 = (bf16[52,128,128]{2,1,0:T(8,128)(2,1)}, bf16[52,128,128]{2,1,0:T(8,128)(2,1)S(1)}, u32[]{:S(2)}) copy-start(bf16[52,128,128]{2,1,0:T(8,128)(2,1)S(1)} %get-tuple-element.36) | copy-start | bytes 5111812
  19.2 36.8 %collective-permute-start.4 = (bf16[64,128,128]{2,1,0:T(8,128)(2,1)}, bf16[64,128,128]{2,1,0:T(8,128)(2,1)S(1)}, u32[]{:S(2)}, u32[]{:S(2)}) collective-permute-start(bf16[64,128,128]{2,1,0:T(8,128)(2,1)} %get-tuple-element.37), channel_id=1, source_target_pairs={{0,1},{1,0},{2,3},{3,2},{4,5},{5,4},{6,7},{7,6},{8,9},{9,8},{10,11... | collective-permute-start | bytes 6291464 | tf_op jit(solution)/shard_map/ppermute | solution.py:537
  31.3 24.6 %collective-permute-start.6 = (bf16[52,128,128]{2,1,0:T(8,128)(2,1)}, bf16[52,128,128]{2,1,0:T(8,128)(2,1)}, u32[]{:S(2)}, u32[]{:S(2)}) collective-permute-start(bf16[52,128,128]{2,1,0:T(8,128)(2,1)} %collective-permute-done.5.refs_1_), channel_id=1, source_target_pairs={{0,1},{1,0},{2,3},{3,2},{4,5},{5,4},{6,7},{7,6},{8,9},{9,8},{10,11... | collective-permute-start | bytes 5111816 | tf_op jit(solution)/shard_map/ppermute | solution.py:537
  31.3 30.8 %collective-permute-start.7 = (bf16[52,128,128]{2,1,0:T(8,128)(2,1)}, bf16[52,128,128]{2,1,0:T(8,128)(2,1)}, u32[]{:S(2)}, u32[]{:S(2)}) collective-permute-start(bf16[52,128,128]{2,1,0:T(8,128)(2,1)} %get-tuple-element.39), channel_id=1, source_target_pairs={{1,3},{2,0},{3,5},{4,2},{5,7},{6,4},{7,9},{8,6},{9,11},{10,8},{11,... | collective-permute-start | bytes 5111816 | tf_op jit(solution)/shard_map/ppermute | solution.py:537
  43.5 2.2 %copy-start.1 = (bf16[128,128,128]{2,1,0:T(8,128)(2,1)S(1)}, bf16[128,128,128]{2,1,0:T(8,128)(2,1)}, u32[]{:S(2)}) copy-start(bf16[128,128,128]{2,1,0:T(8,128)(2,1)} %src.3) | copy-start | bytes 12582916
  55.9 6.3 %copy-start.5 = (bf16[52,128,128]{2,1,0:T(8,128)(2,1)S(1)}, bf16[52,128,128]{2,1,0:T(8,128)(2,1)}, u32[]{:S(2)}) copy-start(bf16[52,128,128]{2,1,0:T(8,128)(2,1)} %copy-done.4) | copy-start | bytes 5111812
  62.1 4.0 %collective-permute-start.8 = (bf16[52,128,128]{2,1,0:T(8,128)(2,1)}, bf16[52,128,128]{2,1,0:T(8,128)(2,1)S(1)}, u32[]{:S(2)}, u32[]{:S(2)}) collective-permute-start(bf16[52,128,128]{2,1,0:T(8,128)(2,1)} %collective-permute-done.7.refs_0_), channel_id=1, source_target_pairs={{0,1},{1,0},{2,3},{3,2},{4,5},{5,4},{6,7},{7,6},{8,9},{9,8},{10,11... | collective-permute-start | bytes 5111816 | tf_op jit(solution)/shard_map/ppermute | solution.py:537
  62.2 27.9 %collective-permute-start.3 = (bf16[52,128,128]{2,1,0:T(8,128)(2,1)S(1)}, bf16[52,128,128]{2,1,0:T(8,128)(2,1)S(1)}, u32[]{:S(2)}, u32[]{:S(2)}) collective-permute-start(bf16[52,128,128]{2,1,0:T(8,128)(2,1)S(1)} %copy-done.5), channel_id=1, source_target_pairs={{0,2},{2,4},{3,1},{4,6},{5,3},{6,8},{7,5},{8,10},{9,7},{10,12},{11... | collective-permute-start | bytes 5111816 | tf_op jit(solution)/shard_map/ppermute | solution.py:537
  64.1 30.2 %collective-permute-start.2 = (bf16[12,128,128]{2,1,0:T(8,128)(2,1)S(1)}, bf16[12,128,128]{2,1,0:T(8,128)(2,1)S(1)}, u32[]{:S(2)}, u32[]{:S(2)}) collective-permute-start(bf16[12,128,128]{2,1,0:T(8,128)(2,1)S(1)} %get-tuple-element.35), channel_id=1, source_target_pairs={{0,2},{2,4},{3,1},{4,6},{5,3},{6,8},{7,5},{8,10},{9,7},{10,12},{11... | collective-permute-start | bytes 1179656 | tf_op jit(solution)/shard_map/ppermute | solution.py:537
